TPU v7x, 32 devices: a whole 2x2x4 slice. The times are simulated.
32 devices in a mesh: fsdp: 4 (over y, x), tenant: 4 (over z), dp: 2 (over core).
Axes of the slice: x: 2, y: 2, z: 4, core: 2. Of those that a mesh axis runs over, the one named last changes fastest.
Arguments:
- tokens: bfloat16 [3072, 5120], P(('fsdp', 'dp'), 'tenant'), may hold values from -6 to 6
- block_tenant_index: int32 [48], P(('fsdp', 'dp')), may hold values from 0 to 7
- ranks: int32 [8], replicated, may hold values from 16 to 64, as said below
- frozen_up_weight: bfloat16 [5120, 14336], P(('fsdp', 'dp'), 'tenant'), may hold values from -0.078125 to 0.078125
- tenant_down_adapters: bfloat16 [8, 64, 5120], P('tenant'), may hold values from -0.078125 to 0.078125
- tenant_up_adapters: bfloat16 [8, 64, 14336], P('tenant'), may hold values from -0.75 to 0.75
- cotangent: bfloat16 [3072, 14336], P(('fsdp', 'dp'), 'tenant'), may hold values from -6 to 6
Outputs:
- hidden_out: bfloat16 [3072, 14336], P(('fsdp', 'dp'), 'tenant')
- grad_tokens: bfloat16 [3072, 5120], P(('fsdp', 'dp'), 'tenant')
- grad_down: float32 [8, 64, 5120], P('dp', None, 'tenant')
- grad_up: float32 [8, 64, 14336], P('dp', None, 'tenant')
Inputs may be any that keep to these rules, and one draw needn't show every extreme that they name: `ranks`: multiples of 16; some tenant has rank 64.
All inputs are finite; a program needn't handle non-finite values.
Results may differ from a plain program's by a relative error of at most 0.0034.
Values may be sent and summed in bfloat16 or wider, within the bound.
No kernel may reach another device: no remote copies, remote signals or barrier semaphores. Data moves between devices by JAX's collectives and lax.ppermute only.
A program may use at most 128 MiB of HBM per device.

v0:
```python
import jax
import jax.numpy as jnp
from jax import lax
from jax.sharding import PartitionSpec as P

BLOCK = 64
alpha_scale = 32.0


def make_gain(block_tenant_index, ranks, rows, largest_rank):
    tenants = ranks.shape[0]
    rows_tenant = jnp.repeat(block_tenant_index, BLOCK, total_repeat_length=rows)
    columns = jnp.arange(tenants * largest_rank, dtype=jnp.int32)
    col_tenant = columns // largest_rank
    col_slot = columns % largest_rank
    ranks_col = jnp.repeat(ranks, largest_rank, total_repeat_length=tenants * largest_rank)
    keep = (rows_tenant[:, None] == col_tenant[None, :]) & (col_slot[None, :] < ranks_col[None, :])
    scale_col = alpha_scale / ranks_col.astype(jnp.float32)
    return jnp.where(keep, scale_col[None, :], jnp.float32(0.0))


def shards(
    tokens,
    block_tenant_index,
    ranks,
    frozen_up_weight,
    tenant_down_adapters,
    tenant_up_adapters,
    cotangent,
):
    rows = tokens.shape[0]
    local_d = tokens.shape[1]
    local_f = cotangent.shape[1]
    tenants = ranks.shape[0]
    largest_rank = tenant_down_adapters.shape[1]
    gain = make_gain(block_tenant_index, ranks, rows, largest_rank)
    whole = lax.all_gather(tokens, "tenant", axis=1, tiled=True)
    weight = lax.all_gather(frozen_up_weight, ("fsdp", "dp"), axis=0, tiled=True)
    down_part, up_adapter_slice = (
        lax.all_to_all(tenant_down_adapters, "tenant", split_axis=2, concat_axis=0, tiled=True),
        lax.all_to_all(tenant_up_adapters, "tenant", split_axis=2, concat_axis=0, tiled=True),
    )
    local_down = down_part.reshape(tenants * largest_rank, local_d)
    partial_proj = lax.dot_general(
        tokens, local_down, (((1,), (1,)), ((), ())), preferred_element_type=jnp.float32
    )
    proj = lax.psum(partial_proj, "tenant")
    flattened_up = up_adapter_slice.reshape(tenants * largest_rank, local_f)
    adapted = (proj * gain).astype(jnp.bfloat16)
    base = jnp.dot(whole, weight, preferred_element_type=jnp.float32)
    hidden_out = (base + jnp.dot(adapted, flattened_up, preferred_element_type=jnp.float32)).astype(
        jnp.bfloat16
    )
    back_part = lax.dot_general(
        cotangent, flattened_up, (((1,), (1,)), ((), ())), preferred_element_type=jnp.float32
    )
    back = lax.psum(back_part, "tenant")
    adapted_grad = (back * gain).astype(jnp.bfloat16)
    base_back = lax.dot_general(
        cotangent, weight, (((1,), (1,)), ((), ())), preferred_element_type=jnp.float32
    )
    grad_base = lax.psum_scatter(base_back, "tenant", scatter_dimension=1, tiled=True)
    grad_tokens = (
        grad_base + jnp.dot(adapted_grad, local_down, preferred_element_type=jnp.float32)
    ).astype(jnp.bfloat16)
    up_term = lax.dot_general(
        adapted, cotangent, (((0,), (0,)), ((), ())), preferred_element_type=jnp.float32
    )
    down_term = lax.dot_general(
        adapted_grad, tokens, (((0,), (0,)), ((), ())), preferred_element_type=jnp.float32
    )
    up_term = up_term.reshape(tenants, largest_rank, local_f)
    down_term = down_term.reshape(tenants, largest_rank, local_d)
    down_share, up_share = (
        lax.psum_scatter(down_term, "dp", scatter_dimension=0, tiled=True),
        lax.psum_scatter(up_term, "dp", scatter_dimension=0, tiled=True),
    )
    grad_down, grad_up = lax.psum((down_share, up_share), "fsdp")
    return (hidden_out, grad_tokens, grad_down, grad_up)


def solution(mesh):
    return jax.shard_map(
        shards,
        mesh=mesh,
        in_specs=(
            P(("fsdp", "dp"), "tenant"),
            P(("fsdp", "dp")),
            P(),
            P(("fsdp", "dp"), "tenant"),
            P("tenant", None, None),
            P("tenant", None, None),
            P(("fsdp", "dp"), "tenant"),
        ),
        out_specs=(
            P(("fsdp", "dp"), "tenant"),
            P(("fsdp", "dp"), "tenant"),
            P("dp", None, "tenant"),
            P("dp", None, "tenant"),
        ),
        check_vma=False,
    )
```

profile of v0, /device:TPU:0, one launch (start us, length us, event | category | flops | bytes accessed | tf_op | source)
XLA Modules:
  0.0 692.7 jit_solution(15375952981959615952)
XLA Ops:
  8.0 6.4 copy.13
  14.5 4.7 reshape.322
  19.1 6.3 all-to-all-start
  25.5 15.8 %copy.16 = bf16[2,64,14336]{1,0,2:T(2,128)(2,1)} copy(bf16[2,64,14336]{2,1,0:T(8,128)(2,1)} %param.16) | data formatting | bytes 7340032 | tf_op args[5]
  41.3 8.6 %reshape.320 = bf16[4,2,229376]{2,1,0:T(2,128)(2,1)} reshape(bf16[14336,2,64]{2,1,0:T(2,128)(2,1)} %bitcast.77) | data formatting | bytes 7340032
  49.9 7.1 %all-to-all-done = bf16[4,2,81920]{2,1,0:T(2,128)(2,1)} async-done(((bf16[4,2,81920]{2,1,0:T(2,128)(2,1)}), bf16[4,2,81920]{2,1,0:T(2,128)(2,1)}, u32[]{:S(2)}, u32[]{:S(2)}) %all-to-all-start) | async-done | bytes 1310752 | tf_op jit(solution)/shard_map/all_to_all | solution.py:40
  56.9 4.8 all-to-all-start.1
  61.8 4.6 reshape.323
  66.4 7.4 %copy.19 = bf16[2,64,4,1280]{3,2,1,0:T(4,128)(2,1)} copy(bf16[2,64,4,1280]{1,0,3,2:T(2,128)(2,1)} %bitcast.82) | data formatting | bytes 2621440 | tf_op jit(solution)/shard_map/all_to_all | solution.py:40
  73.8 1.4 copy.15
  76.3 2.8 fusion.26
  79.1 64.2 %all-to-all-done.1 = bf16[4,2,229376]{2,1,0:T(2,128)(2,1)} async-done(((bf16[4,2,229376]{2,1,0:T(2,128)(2,1)}), bf16[4,2,229376]{2,1,0:T(2,128)(2,1)}, u32[]{:S(2)}, u32[]{:S(2)}) %all-to-all-start.1) | async-done | bytes 3670048 | tf_op jit(solution)/shard_map/all_to_all | solution.py:41
  143.3 8.4 %reshape.321 = bf16[14336,2,64]{2,1,0:T(2,128)(2,1)} reshape(bf16[4,2,229376]{2,1,0:T(2,128)(2,1)} %all-to-all-done.1) | data formatting | bytes 7340032
  151.7 18.7 %copy.20 = bf16[2,64,4,3584]{3,2,1,0:T(4,128)(2,1)} copy(bf16[2,64,4,3584]{1,0,3,2:T(2,128)(2,1)} %bitcast.76) | data formatting | bytes 7340032 | tf_op jit(solution)/shard_map/all_to_all | solution.py:41
  170.4 2.7 copy.18
  173.1 1.8 copy-done.2
  174.9 2.5 fusion.28
  179.7 3.8 fusion.16
  183.5 4.5 compare_select_fusion.2
  188.9 56.8 %all-reduce.5.cloned.1.call-done = (f32[384,512]{1,0:T(8,128)}, f32[384,512]{1,0:T(8,128)}) async-done(((f32[384,512]{1,0:T(8,128)}, f32[384,512]{1,0:T(8,128)}), (f32[384,512]{1,0:T(8,128)}, f32[384,512]{1,0:T(8,128)})) %all-reduce.5.cloned.1.call-update) | async-done | bytes 1572880 | tf_op jit(solution)/shard_map/psum | solution.py:47
  245.7 4.0 fusion.17
  249.8 7.1 %fusion.20 = f32[512,3584]{1,0:T(8,128)} fusion(bf16[384,3584]{1,0:T(8,128)(2,1)S(1)} %copy-done, f32[384,512]{1,0:T(8,128)S(1)} %copy-done.5, f32[512]{0:T(512)S(1)} %convert_divide_fusion, s32[512]{0:T(512)S(1)} %add_select_fusion, s32[384]{0:T(512)S(1)} %and_select_fusion, pred[512]{0:T(512)(128)(4,1)S(1)} %get-tuple-element.32), kind=kOutput, calls=%fused_computation.52 | convolution fusion | flops 1410269184 | bytes 10885120 | tf_op jit(solution)/shard_map/dot_general | solution.py:66
  257.7 96.2 %all-gather.5.cloned.1.call-done = bf16[5120,3584]{1,0:T(8,128)(2,1)} async-done(((bf16[640,3584]{1,0:T(8,128)(2,1)}), bf16[5120,3584]{1,0:T(8,128)(2,1)}) %all-gather.5.cloned.1.call-update) | async-done | bytes 36700176 | tf_op jit(solution)/shard_map/all_gather | solution.py:38
  353.9 22.1 %fusion.27 = f32[384,5120]{1,0:T(8,128)} fusion(bf16[384,3584]{1,0:T(8,128)(2,1)S(1)} %copy-done, bf16[5120,3584]{1,0:T(8,128)(2,1)} %all-gather.5.cloned.1.call-done), kind=kOutput, calls=%fused_computation.57 | convolution fusion | flops 14092861440 | bytes 47316992 | tf_op jit(solution)/shard_map/dot_general | solution.py:59
  376.6 139.9 %all-gather.3.cloned.1.call-done = bf16[384,5120]{1,0:T(8,128)(2,1)} async-done(((bf16[384,1280]{1,0:T(8,128)(2,1)}), bf16[384,5120]{1,0:T(8,128)(2,1)}) %all-gather.3.cloned.1.call-update) | async-done | bytes 3932176 | tf_op jit(solution)/shard_map/all_gather | solution.py:37
  516.5 23.5 %fusion.25 = f32[384,3584]{1,0:T(8,128)} fusion(bf16[384,5120]{1,0:T(8,128)(2,1)} %all-gather.3.cloned.1.call-done, bf16[5120,3584]{1,0:T(8,128)(2,1)} %all-gather.5.cloned.1.call-done), kind=kOutput, calls=%fused_computation.55 | convolution fusion | flops 14092861440 | bytes 46137344 | tf_op jit(solution)/shard_map/dot_general | solution.py:50
  540.0 7.0 %fusion = bf16[384,3584]{1,0:T(8,128)(2,1)} fusion(f32[384,3584]{1,0:T(8,128)} %fusion.25, bf16[512,3584]{1,0:T(8,128)(2,1)} %bitcast.79, f32[384,512]{1,0:T(8,128)S(1)} %copy-done.5, f32[512]{0:T(512)S(1)} %convert_divide_fusion, s32[512]{0:T(512)S(1)} %add_select_fusion, s32[384]{0:T(512)S(1)} %and_select_fusion, pred[512]{0:T(512)(128)(4,1)S(1)} %get-tuple-element.32), kind=kOutput, calls=%fused_computation.1 | convolution fusion | flops 1413021696 | bytes 12720128 | tf_op jit(solution)/shard_map/dot_general | solution.py:51
  547.0 10.7 %reduce-scatter.4.cloned.1.call-done = f32[384,1280]{1,0:T(8,128)} async-done(((f32[384,5120]{1,0:T(8,128)}), f32[384,1280]{1,0:T(8,128)}) %reduce-scatter.4.cloned.1.call-update) | async-done | bytes 1966096 | tf_op jit(solution)/shard_map/reduce_scatter | solution.py:62
  557.7 3.3 fusion.1
  561.0 117.8 %all-reduce.7.cloned.1.call-done = (f32[4,64,1280]{2,1,0:T(8,128)}, f32[4,64,3584]{2,1,0:T(8,128)}) async-done(((f32[4,64,1280]{2,1,0:T(8,128)}, f32[4,64,3584]{2,1,0:T(8,128)}), (f32[4,64,1280]{2,1,0:T(8,128)}, f32[4,64,3584]{2,1,0:T(8,128)})) %all-reduce.7.cloned.1.call-update) | async-done | bytes 4980752 | tf_op jit(solution)/shard_map/psum | solution.py:78
  678.8 2.6 copy.29
  681.4 4.1 copy.30
  (48 shorter events, 5.6 us)
Async XLA Ops:
  8.0 166.9 %copy-start = (bf16[384,3584]{1,0:T(8,128)(2,1)S(1)}, bf16[384,3584]{1,0:T(8,128)(2,1)}, u32[]{:S(2)}) copy-start(bf16[384,3584]{1,0:T(8,128)(2,1)} %param.17) | copy-start | bytes 8257540
  19.1 37.8 %all-to-all-start = ((bf16[4,2,81920]{2,1,0:T(2,128)(2,1)}), bf16[4,2,81920]{2,1,0:T(2,128)(2,1)}, u32[]{:S(2)}, u32[]{:S(2)}) async-start(bf16[4,2,81920]{2,1,0:T(2,128)(2,1)} %reshape.322), calls=%async_computation | async-start | bytes 2621440 | tf_op jit(solution)/shard_map/all_to_all | solution.py:40
  56.9 86.3 %all-to-all-start.1 = ((bf16[4,2,229376]{2,1,0:T(2,128)(2,1)}), bf16[4,2,229376]{2,1,0:T(2,128)(2,1)}, u32[]{:S(2)}, u32[]{:S(2)}) async-start(bf16[4,2,229376]{2,1,0:T(2,128)(2,1)} %reshape.320), calls=%async_computation.1 | async-start | bytes 7340032 | tf_op jit(solution)/shard_map/all_to_all | solution.py:41
  61.8 184.0 %all-reduce.5.cloned.1.call-start = ((), (), s32[]{:S(2)}) async-start(), calls=%async_computation.10 | async-start | bytes 3145728 | tf_op jit(solution)/shard_map/psum | solution.py:47
  75.3 1.1 copy-start.3
  173.1 1.8 copy-start.2
  177.4 0.7 copy-start.8
  177.4 1.4 copy-start.7
  177.4 2.1 copy-start.10
  177.4 2.2 copy-start.9
  177.5 176.5 %all-gather.5.cloned.1.call-start = ((), (), s32[]{:S(2)}) async-start(), calls=%async_computation.6 | async-start | bytes 41287680 | tf_op jit(solution)/shard_map/all_gather | solution.py:38
  178.0 198.0 %reduce-scatter.6.cloned.1.call-start = ((), (), s32[]{:S(2)}) async-start(), calls=%async_computation.8 | async-start | bytes 3932160 | tf_op jit(solution)/shard_map/reduce_scatter | solution.py:75
  245.7 4.1 copy-start.5
  249.7 126.4 %reduce-scatter.8.cloned.1.call-start = ((), (), s32[]{:S(2)}) async-start(), calls=%async_computation.9 | async-start | bytes 11010048 | tf_op jit(solution)/shard_map/reduce_scatter | solution.py:76
  256.9 259.6 %all-gather.3.cloned.1.call-start = ((), (), s32[]{:S(2)}) async-start(), calls=%async_computation.5 | async-start | bytes 4915200 | tf_op jit(solution)/shard_map/all_gather | solution.py:37
  257.5 300.2 %reduce-scatter.4.cloned.1.call-start = ((), (), s32[]{:S(2)}) async-start(), calls=%async_computation.7 | async-start | bytes 9830400 | tf_op jit(solution)/shard_map/reduce_scatter | solution.py:62
  376.0 302.8 %all-reduce.7.cloned.1.call-start = ((), (), s32[]{:S(2)}) async-start(), calls=%async_computation.11 | async-start | bytes 9961472 | tf_op jit(solution)/shard_map/psum | solution.py:78
  540.0 17.8 %copy-start.4 = (bf16[4,2,64,1280]{3,2,1,0:T(8,128)(2,1)S(1)}, bf16[4,2,64,1280]{3,2,1,0:T(8,128)(2,1)}, u32[]{:S(2)}) copy-start(bf16[4,2,64,1280]{3,2,1,0:T(8,128)(2,1)} %copy-done.3) | copy-start | bytes 3932164
  540.0 17.8 %copy-start.6 = (f32[384,512]{1,0:T(8,128)S(1)}, f32[384,512]{1,0:T(8,128)}, u32[]{:S(2)}) copy-start(f32[384,512]{1,0:T(8,128)} %get-tuple-element.29) | copy-start | bytes 2359300
  678.8 6.8 copy-start.1
Sparse Core Ops, SparseCore 0:
  177.6 68.0 all-reduce.4
  249.9 16.8 reduce-scatter.5
  269.1 17.2 reduce-scatter.7
  376.1 181.5 reduce-scatter.3
  561.2 117.5 all-reduce.6
Sparse Core Ops, SparseCore 1:
  179.9 174.0 all-gather.4
  355.4 161.1 all-gather.2
where the time goes:
time: 695 us; the launch traced here: 693 us
  waiting for transfers between devices  494 us (71%)
  local copies, waits for them, and re-layouts  89.8 us (13%)
  matrix products  72.2 us (10%)
  between operations  15.4 us (2%)
  starting transfers between devices  11.6 us (2%)
  other arithmetic  9.35 us (1%)
    all_gather x1, waiting for transfers between devices, shards(): whole = lax.all_gather(tokens, 'tenant', axis=1, tiled=True)  140 us
    psum x1, waiting for transfers between devices, shards(): grad_down, grad_up = lax.psum((down_share, up_share), 'fsdp')  118 us
    all_gather x1, waiting for transfers between devices, shards(): lax.all_gather(frozen_up_weight, ('fsdp', 'dp'), axis=0, tiled=True)  96.2 us
    all_to_all x1, waiting for transfers between devices, shards(): lax.all_to_all(tenant_up_adapters, 'tenant', split_axis=2, concat_axis=0,...  64.2 us
    unnamed x30, local copies, waits for them, and re-layouts  58.2 us
    psum x1, waiting for transfers between devices, shards(): proj = lax.psum(partial_proj, 'tenant')  56.8 us
    dot_general x1, matrix products, shards(): base = jnp.dot(whole, weight, preferred_element_type=jnp.float32)  23.5 us
    dot_general x1, matrix products, shards(): lax.dot_general(cotangent, weight, (((1,), (1,)), ((), ())), preferred_el...  22.1 us
  transfers between devices with their start and end apart: 9, of which 7 were waited for; matrix products, arithmetic and copies ran while one was open for 17% of the time, Pallas kernels for 0%

commit v1 on v0

--- a/solution.py
+++ b/solution.py
@@ -34,7 +34,8 @@
     tenants = ranks.shape[0]
     largest_rank = tenant_down_adapters.shape[1]
     gain = make_gain(block_tenant_index, ranks, rows, largest_rank)
-    whole = lax.all_gather(tokens, "tenant", axis=1, tiled=True)
+    shards_2 = lax.all_gather(tokens, "tenant")
+    whole = jnp.concatenate(shards_2, axis=1)
     weight = lax.all_gather(frozen_up_weight, ("fsdp", "dp"), axis=0, tiled=True)
     down_part, up_adapter_slice = (
         lax.all_to_all(tenant_down_adapters, "tenant", split_axis=2, concat_axis=0, tiled=True),

time: 695 us -> 695 us (level)
  transfers between devices with their start and end apart: 9 -> 9, of which waited for: 7 -> 7; matrix products, arithmetic and copies ran while one was open for 17% -> 18% of each run, Pallas kernels for 0% -> 0%
where the time goes in v1:
time: 695 us; the launch traced here: 693 us
  waiting for transfers between devices  488 us (70%)
  local copies, waits for them, and re-layouts  96.1 us (14%)
  matrix products  72.6 us (10%)
  between operations  15.4 us (2%)
  starting transfers between devices  11.6 us (2%)
  other arithmetic  9.35 us (1%)
    all_gather x1, waiting for transfers between devices, shards(): shards_2 = lax.all_gather(tokens, 'tenant')  140 us
    psum x1, waiting for transfers between devices, shards(): grad_down, grad_up = lax.psum((down_share, up_share), 'fsdp')  118 us
    all_gather x1, waiting for transfers between devices, shards(): lax.all_gather(frozen_up_weight, ('fsdp', 'dp'), axis=0, tiled=True)  96.2 us
    all_to_all x1, waiting for transfers between devices, shards(): lax.all_to_all(tenant_up_adapters, 'tenant', split_axis=2, concat_axis=0,...  64.2 us
    unnamed x30, local copies, waits for them, and re-layouts  58.2 us
    psum x1, waiting for transfers between devices, shards(): proj = lax.psum(partial_proj, 'tenant')  56.8 us
    dot_general x1, matrix products, shards(): base = jnp.dot(whole, weight, preferred_element_type=jnp.float32)  23.8 us
    dot_general x1, matrix products, shards(): lax.dot_general(cotangent, weight, (((1,), (1,)), ((), ())), preferred_el...  22.1 us
  transfers between devices with their start and end apart: 9, of which 7 were waited for; matrix products, arithmetic and copies ran while one was open for 18% of the time, Pallas kernels for 0%

profile of v1, /device:TPU:0, one launch (start us, length us, event | category | flops | bytes accessed | tf_op | source)
XLA Modules:
  0.0 692.7 jit_solution(10970325565534262289)
XLA Ops:
  8.0 6.4 copy.15
  14.5 4.7 reshape.331
  19.1 6.3 all-to-all-start
  25.5 15.8 %copy.18 = bf16[2,64,14336]{1,0,2:T(2,128)(2,1)} copy(bf16[2,64,14336]{2,1,0:T(8,128)(2,1)} %param.16) | data formatting | bytes 7340032 | tf_op args[5]
  41.3 8.6 %reshape.329 = bf16[4,2,229376]{2,1,0:T(2,128)(2,1)} reshape(bf16[14336,2,64]{2,1,0:T(2,128)(2,1)} %bitcast.81) | data formatting | bytes 7340032
  49.9 7.1 %all-to-all-done = bf16[4,2,81920]{2,1,0:T(2,128)(2,1)} async-done(((bf16[4,2,81920]{2,1,0:T(2,128)(2,1)}), bf16[4,2,81920]{2,1,0:T(2,128)(2,1)}, u32[]{:S(2)}, u32[]{:S(2)}) %all-to-all-start) | async-done | bytes 1310752 | tf_op jit(solution)/shard_map/all_to_all | solution.py:41
  56.9 4.8 all-to-all-start.1
  61.8 4.6 reshape.332
  66.4 7.4 %copy.21 = bf16[2,64,4,1280]{3,2,1,0:T(4,128)(2,1)} copy(bf16[2,64,4,1280]{1,0,3,2:T(2,128)(2,1)} %bitcast.86) | data formatting | bytes 2621440 | tf_op jit(solution)/shard_map/all_to_all | solution.py:41
  76.3 2.8 fusion.26
  79.1 64.2 %all-to-all-done.1 = bf16[4,2,229376]{2,1,0:T(2,128)(2,1)} async-done(((bf16[4,2,229376]{2,1,0:T(2,128)(2,1)}), bf16[4,2,229376]{2,1,0:T(2,128)(2,1)}, u32[]{:S(2)}, u32[]{:S(2)}) %all-to-all-start.1) | async-done | bytes 3670048 | tf_op jit(solution)/shard_map/all_to_all | solution.py:42
  143.3 8.4 %reshape.330 = bf16[14336,2,64]{2,1,0:T(2,128)(2,1)} reshape(bf16[4,2,229376]{2,1,0:T(2,128)(2,1)} %all-to-all-done.1) | data formatting | bytes 7340032
  151.7 18.7 %copy.22 = bf16[2,64,4,3584]{3,2,1,0:T(4,128)(2,1)} copy(bf16[2,64,4,3584]{1,0,3,2:T(2,128)(2,1)} %bitcast.80) | data formatting | bytes 7340032 | tf_op jit(solution)/shard_map/all_to_all | solution.py:42
  170.4 2.7 copy.20
  173.1 1.8 copy-done.2
  174.9 2.5 fusion.28
  179.7 3.8 fusion.16
  183.5 4.5 compare_select_fusion.2
  188.9 56.8 %all-reduce.5.cloned.1.call-done = (f32[384,512]{1,0:T(8,128)}, f32[384,512]{1,0:T(8,128)}) async-done(((f32[384,512]{1,0:T(8,128)}, f32[384,512]{1,0:T(8,128)}), (f32[384,512]{1,0:T(8,128)}, f32[384,512]{1,0:T(8,128)})) %all-reduce.5.cloned.1.call-update) | async-done | bytes 1572880 | tf_op jit(solution)/shard_map/psum | solution.py:48
  245.7 4.0 fusion.17
  249.8 7.1 %fusion.20 = f32[512,3584]{1,0:T(8,128)} fusion(bf16[384,3584]{1,0:T(8,128)(2,1)S(1)} %copy-done, f32[384,512]{1,0:T(8,128)S(1)} %copy-done.5, f32[512]{0:T(512)S(1)} %convert_divide_fusion, s32[512]{0:T(512)S(1)} %add_select_fusion, s32[384]{0:T(512)S(1)} %and_select_fusion, pred[512]{0:T(512)(128)(4,1)S(1)} %get-tuple-element.32), kind=kOutput, calls=%fused_computation.52 | convolution fusion | flops 1410269184 | bytes 10885120 | tf_op jit(solution)/shard_map/dot_general | solution.py:67
  257.7 96.2 %all-gather.4.cloned.1.call-done = bf16[5120,3584]{1,0:T(8,128)(2,1)} async-done(((bf16[640,3584]{1,0:T(8,128)(2,1)}), bf16[5120,3584]{1,0:T(8,128)(2,1)}) %all-gather.4.cloned.1.call-update) | async-done | bytes 36700176 | tf_op jit(solution)/shard_map/all_gather | solution.py:39
  353.9 22.1 %fusion.27 = f32[384,5120]{1,0:T(8,128)} fusion(bf16[384,3584]{1,0:T(8,128)(2,1)S(1)} %copy-done, bf16[5120,3584]{1,0:T(8,128)(2,1)} %all-gather.4.cloned.1.call-done), kind=kOutput, calls=%fused_computation.57 | convolution fusion | flops 14092861440 | bytes 47316992 | tf_op jit(solution)/shard_map/dot_general | solution.py:60
  376.6 139.9 %all-gather.6.cloned.1.call-done = bf16[1536,1280]{1,0:T(8,128)(2,1)} async-done(((bf16[384,1280]{1,0:T(8,128)(2,1)}), bf16[1536,1280]{1,0:T(8,128)(2,1)}) %all-gather.6.cloned.1.call-update) | async-done | bytes 3932176 | tf_op jit(solution)/shard_map/all_gather | solution.py:37
  516.5 6.3 copy.14
  522.8 23.8 %fusion.25 = f32[384,3584]{1,0:T(8,128)} fusion(bf16[384,5120]{0,1:T(8,128)(2,1)} %bitcast.92, bf16[5120,3584]{1,0:T(8,128)(2,1)} %all-gather.4.cloned.1.call-done), kind=kOutput, calls=%fused_computation.55 | convolution fusion | flops 14092861440 | bytes 46137344 | tf_op jit(solution)/shard_map/dot_general | solution.py:51
  546.6 7.1 %fusion = bf16[384,3584]{1,0:T(8,128)(2,1)} fusion(f32[384,3584]{1,0:T(8,128)} %fusion.25, bf16[512,3584]{1,0:T(8,128)(2,1)} %bitcast.83, f32[384,512]{1,0:T(8,128)S(1)} %copy-done.5, f32[512]{0:T(512)S(1)} %convert_divide_fusion, s32[512]{0:T(512)S(1)} %add_select_fusion, s32[384]{0:T(512)S(1)} %and_select_fusion, pred[512]{0:T(512)(128)(4,1)S(1)} %get-tuple-element.32), kind=kOutput, calls=%fused_computation.1 | convolution fusion | flops 1413021696 | bytes 12720128 | tf_op jit(solution)/shard_map/dot_general | solution.py:52
  553.7 4.0 reduce-scatter.4.cloned.1.call-done
  557.7 3.3 fusion.1
  561.0 117.8 %all-reduce.7.cloned.1.call-done = (f32[4,64,1280]{2,1,0:T(8,128)}, f32[4,64,3584]{2,1,0:T(8,128)}) async-done(((f32[4,64,1280]{2,1,0:T(8,128)}, f32[4,64,3584]{2,1,0:T(8,128)}), (f32[4,64,1280]{2,1,0:T(8,128)}, f32[4,64,3584]{2,1,0:T(8,128)})) %all-reduce.7.cloned.1.call-update) | async-done | bytes 4980752 | tf_op jit(solution)/shard_map/psum | solution.py:79
  678.8 2.6 copy.31
  681.4 4.1 copy.32
  (49 shorter events, 7.0 us)
Async XLA Ops:
  8.0 166.9 %copy-start = (bf16[384,3584]{1,0:T(8,128)(2,1)S(1)}, bf16[384,3584]{1,0:T(8,128)(2,1)}, u32[]{:S(2)}) copy-start(bf16[384,3584]{1,0:T(8,128)(2,1)} %param.17) | copy-start | bytes 8257540
  19.1 37.8 %all-to-all-start = ((bf16[4,2,81920]{2,1,0:T(2,128)(2,1)}), bf16[4,2,81920]{2,1,0:T(2,128)(2,1)}, u32[]{:S(2)}, u32[]{:S(2)}) async-start(bf16[4,2,81920]{2,1,0:T(2,128)(2,1)} %reshape.331), calls=%async_computation | async-start | bytes 2621440 | tf_op jit(solution)/shard_map/all_to_all | solution.py:41
  56.9 86.3 %all-to-all-start.1 = ((bf16[4,2,229376]{2,1,0:T(2,128)(2,1)}), bf16[4,2,229376]{2,1,0:T(2,128)(2,1)}, u32[]{:S(2)}, u32[]{:S(2)}) async-start(bf16[4,2,229376]{2,1,0:T(2,128)(2,1)} %reshape.329), calls=%async_computation.1 | async-start | bytes 7340032 | tf_op jit(solution)/shard_map/all_to_all | solution.py:42
  61.8 184.0 %all-reduce.5.cloned.1.call-start = ((), (), s32[]{:S(2)}) async-start(), calls=%async_computation.10 | async-start | bytes 3145728 | tf_op jit(solution)/shard_map/psum | solution.py:48
  75.3 1.1 copy-start.3
  173.1 1.8 copy-start.2
  177.4 0.7 copy-start.8
  177.4 1.4 copy-start.7
  177.4 2.1 copy-start.10
  177.4 2.2 copy-start.9
  177.5 176.5 %all-gather.4.cloned.1.call-start = ((), (), s32[]{:S(2)}) async-start(), calls=%async_computation.5 | async-start | bytes 41287680 | tf_op jit(solution)/shard_map/all_gather | solution.py:39
  178.0 198.0 %reduce-scatter.6.cloned.1.call-start = ((), (), s32[]{:S(2)}) async-start(), calls=%async_computation.7 | async-start | bytes 3932160 | tf_op jit(solution)/shard_map/reduce_scatter | solution.py:76
  245.7 4.1 copy-start.5
  249.7 126.4 %reduce-scatter.8.cloned.1.call-start = ((), (), s32[]{:S(2)}) async-start(), calls=%async_computation.8 | async-start | bytes 11010048 | tf_op jit(solution)/shard_map/reduce_scatter | solution.py:77
  256.9 259.6 %all-gather.6.cloned.1.call-start = ((), (), s32[]{:S(2)}) async-start(), calls=%async_computation.9 | async-start | bytes 4915200 | tf_op jit(solution)/shard_map/all_gather | solution.py:37
  257.5 300.2 %reduce-scatter.4.cloned.1.call-start = ((), (), s32[]{:S(2)}) async-start(), calls=%async_computation.6 | async-start | bytes 9830400 | tf_op jit(solution)/shard_map/reduce_scatter | solution.py:63
  376.0 302.8 %all-reduce.7.cloned.1.call-start = ((), (), s32[]{:S(2)}) async-start(), calls=%async_computation.11 | async-start | bytes 9961472 | tf_op jit(solution)/shard_map/psum | solution.py:79
  546.6 11.1 %copy-start.4 = (bf16[4,2,64,1280]{3,2,1,0:T(8,128)(2,1)S(1)}, bf16[4,2,64,1280]{3,2,1,0:T(8,128)(2,1)}, u32[]{:S(2)}) copy-start(bf16[4,2,64,1280]{3,2,1,0:T(8,128)(2,1)} %copy-done.3) | copy-start | bytes 3932164
  546.6 11.1 %copy-start.6 = (f32[384,512]{1,0:T(8,128)S(1)}, f32[384,512]{1,0:T(8,128)}, u32[]{:S(2)}) copy-start(f32[384,512]{1,0:T(8,128)} %get-tuple-element.29) | copy-start | bytes 2359300
  678.8 6.8 copy-start.1
Sparse Core Ops, SparseCore 0:
  177.6 68.0 all-reduce.4
  249.9 16.8 reduce-scatter.5
  269.1 17.2 reduce-scatter.7
  376.1 181.5 reduce-scatter.3
  561.2 117.5 all-reduce.6
Sparse Core Ops, SparseCore 1:
  179.9 174.0 all-gather.3
  355.4 161.1 all-gather.5
